TPU v7x, 32 devices: a whole 2x2x4 slice. The times are simulated.
32 devices in a mesh: row: 4 (over y, core), col: 4 (over z), depth: 2 (over x).
Axes of the slice: x: 2, y: 2, z: 4, core: 2. Of those that a mesh axis runs over, the one named last changes fastest.
Arguments:
- diag_block: float32 [512, 512], P(('row', 'col', 'depth')), as said below
- panel_rows: float32 [32256, 512], P(('row', 'col', 'depth')), may hold values from -2 to 2
- trailing: float32 [32256, 1024], P(('row', 'depth'), 'col'), may hold values from -6 to 6
Outputs:
- diag_factor: float32 [512, 512], P(('row', 'col', 'depth'))
- panel_factor: float32 [32256, 512], P(('row', 'col', 'depth'))
- updated: float32 [32256, 1024], P(('row', 'depth'), 'col')
Inputs may be any that keep to these rules, and one draw needn't show every extreme that they name: `diag_block`: symmetric positive definite.
All inputs are finite; a program needn't handle non-finite values.
Results may differ from a plain program's by a relative error of at most 0.000062.
Values sent between devices are 32-bit elements; how exact they have to be, the bound alone decides.
A program may use at most 64 MiB of HBM per device.

v0:
```python
import jax
import jax.numpy as jnp
from jax import lax
from jax.sharding import PartitionSpec as P

highest = lax.Precision.HIGHEST


def spread(value, axis, source):
    kept = jnp.where(lax.axis_index(axis) == source, value, 0).astype(value.dtype)
    return lax.psum(kept, axis)


def rows_times(left, right):
    return lax.dot_general(
        left, right, (((1,), (1,)), ((), ())), precision=highest, preferred_element_type=jnp.float32
    )


def body(diag_block, panel_rows, trailing):
    whole_diag = lax.all_gather(diag_block, ("row", "col", "depth"), axis=0, tiled=True)
    factor = jnp.linalg.cholesky(whole_diag)
    position = (
        lax.axis_index("row") * lax.axis_size("col") + lax.axis_index("col")
    ) * lax.axis_size("depth") + lax.axis_index("depth")
    mine = diag_block.shape[0]
    own_factor = lax.dynamic_slice_in_dim(factor, position * mine, mine, 0)
    solved = jax.scipy.linalg.solve_triangular(factor, panel_rows.T, lower=True).T
    win_rows = trailing.shape[1]
    own_rows = trailing.shape[0]
    block_row = lax.all_gather(solved, ("col", "depth"), axis=0, tiled=True)
    owned = lax.dynamic_slice_in_dim(block_row, lax.axis_index("depth") * own_rows, own_rows, 0)
    local_window = lax.dynamic_slice_in_dim(
        block_row, lax.axis_index("col") * win_rows, win_rows, 0
    )
    full_window = spread(local_window, "row", 0)
    updated = trailing - rows_times(owned, full_window)
    return (own_factor, solved, updated)


def solution(mesh):
    in_specs = (
        P(("row", "col", "depth"), None),
        P(("row", "col", "depth"), None),
        P(("row", "depth"), "col"),
    )
    out_specs = (
        P(("row", "col", "depth"), None),
        P(("row", "col", "depth"), None),
        P(("row", "depth"), "col"),
    )
    return jax.shard_map(body, mesh=mesh, in_specs=in_specs, out_specs=out_specs, check_vma=False)
```

profile of v0, /device:TPU:16, one launch (start us, length us, event | category | flops | bytes accessed | tf_op | source)
XLA Modules:
  0.0 494.1 jit_solution(6985193710742629537)
XLA Ops:
  8.0 56.7 %all-gather.3.cloned.1.call-done = f32[512,512]{1,0:T(8,128)} async-done(((f32[16,512]{1,0:T(8,128)}), f32[512,512]{1,0:T(8,128)}) %all-gather.3.cloned.1.call-update) | async-done | bytes 1048592 | tf_op jit(solution)/shard_map/all_gather | solution.py:21
  64.7 1.6 copy.8
  66.6 11.7 %cholesky.104 = f32[128,128]{1,0:T(8,128)S(1)} custom-call(f32[128,128]{1,0:T(8,128)S(1)} %cholesky.266), custom_call_target="Cholesky" | custom-call | tf_op jit(solution)/shard_map/jit(cholesky)/cholesky | solution.py:22
  78.3 9.8 %custom-call.31 = f32[1,128,128]{1,2,0:T(8,128)S(1)} custom-call(f32[1,128,128]{2,1,0:T(8,128)S(1)} %get-tuple-element.32), custom_call_target="InvertDiagBlocksLowerTriangular" | custom-call | tf_op jit(solution)/shard_map/jit(cholesky)/cholesky | solution.py:22
  89.0 11.7 %cholesky.217 = f32[128,128]{1,0:T(8,128)S(1)} custom-call(f32[128,128]{1,0:T(8,128)S(1)} %cholesky.270), custom_call_target="Cholesky" | custom-call | tf_op jit(solution)/shard_map/jit(cholesky)/cholesky | solution.py:22
  100.7 18.5 %custom-call.32 = f32[1,128,128]{1,2,0:T(8,128)S(1)} custom-call(f32[1,128,128]{2,1,0:T(8,128)S(1)} %get-tuple-element.29), custom_call_target="InvertDiagBlocksLowerTriangular" | custom-call | tf_op jit(solution)/shard_map/jit(cholesky)/cholesky | solution.py:22
  119.8 11.7 %cholesky.238 = f32[128,128]{1,0:T(8,128)S(1)} custom-call(f32[128,128]{1,0:T(8,128)S(1)} %cholesky.275), custom_call_target="Cholesky" | custom-call | tf_op jit(solution)/shard_map/jit(cholesky)/cholesky | solution.py:22
  132.2 9.8 %custom-call.33 = f32[1,128,128]{1,2,0:T(8,128)S(1)} custom-call(f32[1,128,128]{2,1,0:T(8,128)S(1)} %get-tuple-element.26), custom_call_target="InvertDiagBlocksLowerTriangular" | custom-call | tf_op jit(solution)/shard_map/jit(cholesky)/cholesky | solution.py:22
  142.6 11.7 %cholesky.255 = f32[128,128]{1,0:T(8,128)S(1)} custom-call(f32[128,128]{1,0:T(8,128)S(1)} %convolution_subtract_fusion.4), custom_call_target="Cholesky" | custom-call | tf_op jit(solution)/shard_map/jit(cholesky)/cholesky | solution.py:22
  158.8 8.0 %while.1 = (s32[]{:T(128)}, f32[512,512]{1,0:T(8,128)S(1)}, s32[4,2]{0,1:T(2,128)S(1)}, f32[4,128,128]{2,1,0:T(8,128)S(1)}, s32[]{:T(128)}) while((s32[]{:T(128)}, f32[512,512]{1,0:T(8,128)S(1)}, s32[4,2]{0,1:T(2,128)S(1)}, f32[4,128,128]{2,1,0:T(8,128)S(1)}, s32[]{:T(128)}) %tuple.32), condition=%wide.while_cond, body=%wide.while_body.sunk | while | flops 2 | bytes 131189 | solution.py:28
  159.4 1.4 bitcast_dynamic-update-slice_fusion.2
  161.4 1.4 bitcast_dynamic-update-slice_fusion.2
  163.4 1.4 bitcast_dynamic-update-slice_fusion.2
  165.4 1.4 bitcast_dynamic-update-slice_fusion.2
  166.8 39.3 %custom-call.34 = f32[4,128,128]{1,2,0:T(8,128)S(1)} custom-call(f32[4,128,128]{2,1,0:T(8,128)S(1)} %get-tuple-element.10), custom_call_target="InvertDiagBlocksLowerTriangular" | custom-call | tf_op jit(solution)/shard_map/jit(_solve_triangular)/triangular_solve | solution.py:28
  206.2 1.6 fusion.19
  207.8 1.6 convolution_subtract_fusion.1
  210.0 2.0 convolution_subtract_fusion
  212.6 2.5 fusion.11
  215.7 1.4 maximum_bitcast_fusion
  217.2 223.4 %all-gather.5.cloned.1.call-done = f32[8064,512]{1,0:T(8,128)} async-done(((f32[1008,512]{1,0:T(8,128)}), f32[8064,512]{1,0:T(8,128)}) %all-gather.5.cloned.1.call-update) | async-done | bytes 16515088 | tf_op jit(solution)/shard_map/all_gather | solution.py:31
  440.6 1.9 dynamic-slice_select_fusion
  443.2 32.9 %all-reduce.3.cloned.1.call-done = f32[256,512]{1,0:T(8,128)} async-done(((f32[256,512]{1,0:T(8,128)}), f32[256,512]{1,0:T(8,128)}) %all-reduce.3.cloned.1.call-update) | async-done | bytes 524304 | tf_op jit(solution)/shard_map/psum | solution.py:11
  476.1 11.1 %fusion.2 = f32[4032,256]{1,0:T(8,128)} fusion(f32[4032,256]{1,0:T(8,128)} %param.5, f32[256,512]{1,0:T(8,128)} %all-reduce.3.cloned.1.call-done, f32[8064,512]{1,0:T(8,128)} %all-gather.5.cloned.1.call-done, s32[]{:T(128)S(6)} %select_n.23), kind=kOutput, calls=%fused_computation.4 | convolution fusion | flops 6342819840 | bytes 17039364 | tf_op jit(solution)/shard_map/dot_general | solution.py:15
  (42 shorter events, 10.3 us)
Async XLA Ops:
  7.2 57.5 %all-gather.3.cloned.1.call-start = ((), (), s32[]{:S(2)}) async-start(), calls=%async_computation | async-start | bytes 1081344 | tf_op jit(solution)/shard_map/all_gather | solution.py:21
  7.9 432.7 %all-gather.5.cloned.1.call-start = ((), (), s32[]{:S(2)}) async-start(), calls=%async_computation.1 | async-start | bytes 18579456 | tf_op jit(solution)/shard_map/all_gather | solution.py:31
  64.7 1.7 copy-start
  217.1 259.0 %all-reduce.3.cloned.1.call-start = ((), (), s32[]{:S(2)}) async-start(), calls=%async_computation.2 | async-start | bytes 1048576 | tf_op jit(solution)/shard_map/psum | solution.py:11
Sparse Core Ops, SparseCore 0:
  11.0 53.6 all-gather.2
  217.3 223.3 all-gather.4
  443.6 32.4 all-reduce.2
where the time goes:
time: 501 us; the launch traced here: 494 us
  waiting for transfers between devices  314 us (63%)
  other arithmetic  130 us (26%)
  matrix products  22.4 us (4%)
  between operations  17 us (3%)
  local copies, waits for them, and re-layouts  10.3 us (2%)
    all_gather x1, waiting for transfers between devices, body(): block_row = lax.all_gather(solved, ('col', 'depth'), axis=0, tiled=True)  223 us
    another operation x14, other arithmetic, body(): factor = jnp.linalg.cholesky(whole_diag)  87.1 us
    all_gather x1, waiting for transfers between devices, body(): lax.all_gather(diag_block, ('row', 'col', 'depth'), axis=0, tiled=True)  56.7 us
    another operation x3, other arithmetic, body(): jax.scipy.linalg.solve_triangular(factor, panel_rows.T, lower=True)  39.7 us
    psum x1, waiting for transfers between devices, spread(): return lax.psum(kept, axis)  32.9 us
    dot_general x1, matrix products, rows_times(): lax.dot_general(left, right, (((1,), (1,)), ((), ())), precision=highest,...  11.1 us
  transfers between devices with their start and end apart: 3, of which 3 were waited for; matrix products, arithmetic and copies ran while one was open for 0% of the time, Pallas kernels for 0%

commit v1 on v0

v1 whole, which is shorter than its diff:
```python
import functools
import math

import jax
import jax.numpy as jnp
from jax import lax
from jax.experimental import pallas as pl
from jax.experimental.pallas import tpu as pltpu
from jax.sharding import PartitionSpec as P

highest = lax.Precision.HIGHEST
AXES = ("row", "col", "depth")
LANES = 128


def dot(left, right, left_dim, right_dim):
    return lax.dot_general(
        left, right, (((left_dim,), (right_dim,)), ((), ())), precision=highest, preferred_element_type=jnp.float32
    )


def factor_block(block):
    size = block.shape[0]
    lane = lax.broadcasted_iota(jnp.int32, (8, size), 1)
    sub = lax.broadcasted_iota(jnp.int32, (8, size), 0)
    tiles = [block[8 * i : 8 * i + 8, :] for i in range(size // 8)]
    for j in range(size):
        t, s = divmod(j, 8)
        row = tiles[t][s : s + 1, :]
        inverse = 1.0 / row[:, j : j + 1]
        source = jnp.where(lane[0:1] == j, 1.0, row) * inverse
        for i in range(t, size // 8):
            if i == t and s == 7:
                continue
            tile = tiles[i]
            new = jnp.where(lane == j, 0.0, tile) - tile[:, j : j + 1] * source
            tiles[i] = jnp.where(sub > s, new, tile) if i == t else new
    whole = jnp.concatenate(tiles, axis=0)
    r_id = lax.broadcasted_iota(jnp.int32, (size, size), 0)
    c_id = lax.broadcasted_iota(jnp.int32, (size, size), 1)
    pivots = jnp.sum(jnp.where(r_id == c_id, whole, 0.0), axis=1, keepdims=True)
    root = jnp.sqrt(pivots)
    scaled = jnp.where(r_id == c_id, 1.0, whole) / root
    inverse = jnp.where(r_id >= c_id, scaled, 0.0)
    upper = jnp.where(r_id < c_id, scaled, jnp.where(r_id == c_id, root, 0.0))
    return upper.T, inverse


def factor_all(work, low, inv, between=None):
    n = work.shape[0]
    low[...] = jnp.zeros((n, n), jnp.float32)
    inv[...] = jnp.zeros((n, n), jnp.float32)

    def step(k, carry):
        at = pl.ds(pl.multiple_of(k * LANES, LANES), LANES)
        block_low, block_inv = factor_block(work[at, at])
        rows = lax.broadcasted_iota(jnp.int32, (n, LANES), 0)
        panel = jnp.where(rows >= (k + 1) * LANES, dot(work[:, at], block_inv, 1, 1), 0.0)
        work[...] = work[...] - dot(panel, panel, 1, 1)
        left = dot(low[at, :], inv[...], 1, 0)
        low[:, at] = panel
        low[at, at] = block_low
        inv[at, :] = -dot(block_inv, left, 1, 0)
        inv[at, at] = block_inv
        if between is not None:
            between(k)
        return carry

    lax.fori_loop(0, n // LANES, step, 0)


def local_factor(diag_ref, low, inv, work):
    work[...] = diag_ref[...]
    factor_all(work, low, inv)


def factor_call(whole_diag):
    shape = jax.ShapeDtypeStruct(whole_diag.shape, jnp.float32)
    n = whole_diag.shape[0]
    return pl.pallas_call(
        local_factor,
        out_shape=(shape, shape),
        scratch_shapes=[pltpu.VMEM((n, n), jnp.float32)],
        cost_estimate=pl.CostEstimate(flops=400_000 * n, bytes_accessed=12 * n * n, transcendentals=0),
    )(whole_diag)


def spread(value, axis, source):
    kept = jnp.where(lax.axis_index(axis) == source, value, 0).astype(value.dtype)
    return lax.psum(kept, axis)


def body(diag_block, panel_rows, trailing):
    position = (
        lax.axis_index("row") * lax.axis_size("col") + lax.axis_index("col")
    ) * lax.axis_size("depth") + lax.axis_index("depth")
    mine = diag_block.shape[0]
    own_rows, win_rows = trailing.shape
    whole_diag = lax.all_gather(diag_block, AXES, axis=0, tiled=True)
    block_row = lax.all_gather(panel_rows, ("col", "depth"), axis=0, tiled=True)
    owned = lax.dynamic_slice_in_dim(block_row, lax.axis_index("depth") * own_rows, own_rows, 0)
    local_window = lax.dynamic_slice_in_dim(block_row, lax.axis_index("col") * win_rows, win_rows, 0)
    full_window = spread(local_window, "row", 0)
    low, inv = factor_call(whole_diag)
    own_factor = lax.dynamic_slice_in_dim(low, position * mine, mine, 0)
    solved = dot(panel_rows, inv, 1, 1)
    weight = dot(dot(full_window, inv, 1, 1), inv, 1, 0)
    updated = trailing - dot(owned, weight, 1, 1)
    return (own_factor, solved, updated)


def solution(mesh):
    specs = (P(AXES, None), P(AXES, None), P(("row", "depth"), "col"))
    return jax.shard_map(body, mesh=mesh, in_specs=specs, out_specs=specs, check_vma=False)
```

time: 501 us -> 352 us (0.70); the launches traced: 494 us -> 350 us
  other arithmetic: 130 us -> 1.87 us
  waiting for transfers between devices: 314 us -> 257 us
  Pallas kernels: 0 us -> 55.8 us
  local copies, waits for them, and re-layouts: 10.3 us -> 1.47 us
    another operation x17 -> x0, other arithmetic: 127 us -> none  [the longest x14 87.1 us: body(): factor = jnp.linalg.cholesky(whole_diag)]
    pallas_call x0 -> x1, Pallas kernels: none -> 55.8 us  [factor_call(): pl.pallas_call(local_factor, out_shape=(shape, shape), scratch_shapes=[pl...]
    all_gather x2, waiting for transfers between devices: 280 us -> 229 us  [the longest x1 173 us: body(): block_row = lax.all_gather(panel_rows, ('col', 'depth'), axis=0, tiled=True)]
    another operation x13 -> x0, matrix products: 11.3 us -> none  [the longest x7 9.45 us: body(): jax.scipy.linalg.solve_triangular(factor, panel_rows.T, lower=True)]
    dot_general x1 -> x4, matrix products: 11.1 us -> 20 us  [dot(): lax.dot_general(left, right, (((left_dim,), (right_dim,)), ((), ())), pre...]
    another operation x17 -> x0, local copies, waits for them, and re-layouts: 8.06 us -> none
    psum x1, waiting for transfers between devices: 32.9 us -> 27 us  [spread(): return lax.psum(kept, axis)]
  transfers between devices with their start and end apart: 3 -> 3, of which waited for: 3 -> 3; matrix products, arithmetic and copies ran while one was open for 0% -> 2% of each run, Pallas kernels for 0% -> 16%
where the time goes in v1:
time: 352 us; the launch traced here: 350 us
  waiting for transfers between devices  257 us (73%)
  Pallas kernels  55.8 us (16%)
  matrix products  20 us (6%)
  between operations  13.8 us (4%)
    all_gather x1, waiting for transfers between devices, body(): block_row = lax.all_gather(panel_rows, ('col', 'depth'), axis=0, tiled=True)  173 us
    all_gather x1, waiting for transfers between devices, body(): whole_diag = lax.all_gather(diag_block, AXES, axis=0, tiled=True)  56 us
    pallas_call x1, Pallas kernels, factor_call(): pl.pallas_call(local_factor, out_shape=(shape, shape), scratch_shapes=[pl...  55.8 us
    psum x1, waiting for transfers between devices, spread(): return lax.psum(kept, axis)  27 us
    dot_general x4, matrix products, dot(): lax.dot_general(left, right, (((left_dim,), (right_dim,)), ((), ())), pre...  20 us
  transfers between devices with their start and end apart: 3, of which 3 were waited for; matrix products, arithmetic and copies ran while one was open for 2% of the time, Pallas kernels for 16%

profile of v1, /device:TPU:16, one launch (start us, length us, event | category | flops | bytes accessed | tf_op | source)
XLA Modules:
  0.0 350.4 jit_solution(5190713028144259798)
XLA Ops:
  7.2 0.0 copy-start.2
  7.2 0.0 all-gather.3.cloned.1.call-start
  7.2 0.7 all-gather.3.cloned.1.call-update
  7.9 0.0 all-gather.5.cloned.1.call-start
  8.0 0.7 all-gather.5.cloned.1.call-update
  8.7 0.0 all-reduce.2.cloned.1.call-start
  8.7 56.0 %all-gather.3.cloned.1.call-done.diag_ref = f32[512,512]{1,0:T(8,128)} async-done(((f32[16,512]{1,0:T(8,128)}), f32[512,512]{1,0:T(8,128)}) %all-gather.3.cloned.1.call-update) | async-done | bytes 1048592 | tf_op jit(solution)/shard_map/all_gather | solution.py:99
  64.7 55.8 %shard_map.58 = (f32[512,512]{1,0:T(8,128)}, f32[512,512]{1,0:T(8,128)}) custom-call(f32[512,512]{1,0:T(8,128)} %all-gather.3.cloned.1.call-done.diag_ref), custom_call_target="tpu_custom_call" | custom-call | flops 204800000 | bytes 3145728 | tf_op jit(solution)/shard_map/pallas_call | solution.py:80
  120.5 0.0 copy-start.1
  120.5 1.5 constant_dynamic-slice_fusion
  122.0 172.9 %all-gather.5.cloned.1.call-done = f32[8064,512]{1,0:T(8,128)} async-done(((f32[1008,512]{1,0:T(8,128)}), f32[8064,512]{1,0:T(8,128)}) %all-gather.5.cloned.1.call-update) | async-done | bytes 16515088 | tf_op jit(solution)/shard_map/all_gather | solution.py:100
  294.9 1.9 dynamic-slice_select_fusion
  296.8 0.0 all-reduce.2.cloned.1.call-update
  296.8 0.0 copy-done.2
  296.8 5.9 %fusion.6 = f32[1008,512]{1,0:T(8,128)} fusion(f32[1008,512]{1,0:T(8,128)S(1)} %copy-done.2, f32[512,512]{1,0:T(8,128)} %get-tuple-element.6), kind=kOutput, calls=%fused_computation.6 | convolution fusion | flops 3170893824 | bytes 5177344 | tf_op jit(solution)/shard_map/dot_general | solution.py:17
  302.7 27.0 %all-reduce.2.cloned.1.call-done = f32[256,512]{1,0:T(8,128)} async-done(((f32[256,512]{1,0:T(8,128)}), f32[256,512]{1,0:T(8,128)}) %all-reduce.2.cloned.1.call-update) | async-done | bytes 524304 | tf_op jit(solution)/shard_map/psum | solution.py:90
  329.8 0.0 copy-done.1
  329.8 0.0 copy-start
  329.8 2.2 fusion.7
  332.0 1.1 fusion.8
  333.1 0.0 copy-done
  333.1 10.7 %fusion.2 = f32[4032,256]{1,0:T(8,128)} fusion(f32[4032,256]{1,0:T(8,128)S(1)} %copy-done, f32[256,512]{1,0:T(8,128)S(1)} %fusion.8, f32[8064,512]{1,0:T(8,128)} %all-gather.5.cloned.1.call-done, s32[]{:T(128)S(6)} %select_n.18), kind=kOutput, calls=%fused_computation.2 | convolution fusion | flops 6342819840 | bytes 17039364 | tf_op jit(solution)/shard_map/dot_general | solution.py:17
Async XLA Ops:
  7.2 289.6 %copy-start.2 = (f32[1008,512]{1,0:T(8,128)S(1)}, f32[1008,512]{1,0:T(8,128)}, u32[]{:S(2)}) copy-start(f32[1008,512]{1,0:T(8,128)} %param.4) | copy-start | bytes 6193156
  7.2 57.5 %all-gather.3.cloned.1.call-start = ((), (), s32[]{:S(2)}) async-start(), calls=%async_computation | async-start | bytes 1081344 | tf_op jit(solution)/shard_map/all_gather | solution.py:99
  7.9 287.0 %all-gather.5.cloned.1.call-start = ((), (), s32[]{:S(2)}) async-start(), calls=%async_computation.1 | async-start | bytes 18579456 | tf_op jit(solution)/shard_map/all_gather | solution.py:100
  8.7 321.1 %all-reduce.2.cloned.1.call-start = ((), (), s32[]{:S(2)}) async-start(), calls=%async_computation.2 | async-start | bytes 1048576 | tf_op jit(solution)/shard_map/psum | solution.py:90
  120.5 209.3 %copy-start.1 = (f32[512,512]{1,0:T(8,128)S(1)}, f32[512,512]{1,0:T(8,128)}, u32[]{:S(2)}) copy-start(f32[512,512]{1,0:T(8,128)} %get-tuple-element.6) | copy-start | bytes 3145732
  329.8 3.3 copy-start
Sparse Core Ops, SparseCore 0:
  11.0 53.6 all-gather.2
  66.9 227.9 all-gather.4
  297.2 32.4 all-reduce.1

commit v2 on v1

v2 whole, which is shorter than its diff:
```python
import functools
import math

import jax
import jax.numpy as jnp
from jax import lax
from jax.experimental import pallas as pl
from jax.experimental.pallas import tpu as pltpu
from jax.sharding import PartitionSpec as P

highest = lax.Precision.HIGHEST
AXES = ("row", "col", "depth")
LANES = 128


def dot(left, right, left_dim, right_dim):
    return lax.dot_general(
        left, right, (((left_dim,), (right_dim,)), ((), ())), precision=highest, preferred_element_type=jnp.float32
    )


def factor_block(block, halfway=None):
    size = block.shape[0]
    lane = lax.broadcasted_iota(jnp.int32, (8, size), 1)
    sub = lax.broadcasted_iota(jnp.int32, (8, size), 0)
    tiles = [block[8 * i : 8 * i + 8, :] for i in range(size // 8)]
    for j in range(size):
        if halfway is not None and j == size // 2:
            halfway()
        t, s = divmod(j, 8)
        row = tiles[t][s : s + 1, :]
        inverse = 1.0 / row[:, j : j + 1]
        source = jnp.where(lane[0:1] == j, 1.0, row) * inverse
        for i in range(t, size // 8):
            if i == t and s == 7:
                continue
            tile = tiles[i]
            new = jnp.where(lane == j, 0.0, tile) - tile[:, j : j + 1] * source
            tiles[i] = jnp.where(sub > s, new, tile) if i == t else new
    whole = jnp.concatenate(tiles, axis=0)
    r_id = lax.broadcasted_iota(jnp.int32, (size, size), 0)
    c_id = lax.broadcasted_iota(jnp.int32, (size, size), 1)
    pivots = jnp.sum(jnp.where(r_id == c_id, whole, 0.0), axis=1, keepdims=True)
    root = jnp.sqrt(pivots)
    scaled = jnp.where(r_id == c_id, 1.0, whole) / root
    inverse = jnp.where(r_id >= c_id, scaled, 0.0)
    upper = jnp.where(r_id < c_id, scaled, jnp.where(r_id == c_id, root, 0.0))
    return upper.T, inverse


def factor_all(work, low, inv, between=None):
    n = work.shape[0]
    low[...] = jnp.zeros((n, n), jnp.float32)
    inv[...] = jnp.zeros((n, n), jnp.float32)

    def step(k, carry):
        at = pl.ds(pl.multiple_of(k * LANES, LANES), LANES)
        halfway = None if between is None else functools.partial(between, k, 0)
        block_low, block_inv = factor_block(work[at, at], halfway)
        rows = lax.broadcasted_iota(jnp.int32, (n, LANES), 0)
        panel = jnp.where(rows >= (k + 1) * LANES, dot(work[:, at], block_inv, 1, 1), 0.0)
        work[...] = work[...] - dot(panel, panel, 1, 1)
        left = dot(low[at, :], inv[...], 1, 0)
        low[:, at] = panel
        low[at, at] = block_low
        inv[at, :] = -dot(block_inv, left, 1, 0)
        inv[at, at] = block_inv
        if between is not None:
            between(k, 1)
        return carry

    lax.fori_loop(0, n // LANES, step, 0)


def exchange(sizes, cuts, win_units, diag_ref, panel, low, inv, held, window, pieces, work, sems):
    n_r, n_c, n_d = sizes
    total = n_r * n_c * n_d
    half = n_c // 2
    units = panel.shape[0]
    (diag_s, diag_r, ring_s, ring_r, deep_s, deep_r, w1_s, w1_r, w2_s, w2_r, w3_s, w3_r, own_s) = sems
    r, c, d = lax.axis_index("row"), lax.axis_index("col"), lax.axis_index("depth")
    position = (r * n_c + c) * n_d + d

    def remote(src, dst, send, recv, **where):
        return pltpu.make_async_remote_copy(
            src_ref=src,
            dst_ref=dst,
            send_sem=send,
            recv_sem=recv,
            device_id={"row": where.get("row", r), "col": where.get("col", c), "depth": where.get("depth", d)},
            device_id_type=pl.DeviceIdType.MESH,
        )

    def taker(block):
        return lax.div(block * n_d + d, n_c)

    def slot(block):
        return jnp.where(taker(block) == d, block * n_d + d - n_c * d, n_c + block)

    def at(h):
        return pl.ds(cuts[h], cuts[h + 1] - cuts[h])

    def send_diag(k, carry):
        to = lax.rem(position + k, total)
        remote(
            diag_ref, pieces.at[position], diag_s, diag_r,
            row=lax.div(to, n_c * n_d), col=lax.rem(lax.div(to, n_d), n_c), depth=lax.rem(to, n_d),
        ).start()
        return carry

    lax.fori_loop(1, total, send_diag, 0)
    pieces[position] = diag_ref[...]

    def window_parts():
        for p in range(-(-n_c * win_units // units)):
            for b in range(n_c):
                lo, hi = max(b * win_units, p * units), min((b + 1) * win_units, (p + 1) * units)
                if lo < hi:
                    yield p, b, lo, hi - lo

    def part(p, b, lo, count):
        src = panel.at[pl.ds(lo - p * units, count)]
        dst = window.at[pl.ds(lo - b * win_units, count)]
        if p == b * n_d:
            return pltpu.make_async_copy(src, dst, w1_r.at[p])
        return remote(src, dst, w1_s.at[p, b], w1_r.at[p], row=0, col=b, depth=0)

    root = jnp.logical_and(r == 0, d == 0)
    for p, b, lo, count in window_parts():
        @pl.when(position == p)
        def _(p=p, b=b, lo=lo, count=count):
            part(p, b, lo, count).start()

    def to_depth(k):
        return remote(window, window, w2_s.at[k], w2_r, depth=k)

    def to_row(k):
        return remote(window, window, w3_s.at[k], w3_r, row=k)

    def window_second():
        for p, b, lo, count in window_parts():
            @pl.when(jnp.logical_and(root, c == b))
            def _(p=p, b=b, lo=lo, count=count):
                if p == b * n_d:
                    part(p, b, lo, count).wait()
                else:
                    piece = window.at[pl.ds(lo - b * win_units, count)]
                    pltpu.make_async_copy(piece, piece, w1_r.at[p]).wait()

        @pl.when(root)
        def _():
            for k in range(1, n_d):
                to_depth(k).start()

    def window_third():
        @pl.when(jnp.logical_and(r == 0, d != 0))
        def _():
            pltpu.make_async_copy(window, window, w2_r).wait()

        @pl.when(r == 0)
        def _():
            for k in range(1, n_r):
                to_row(k).start()

    def ring(way, s, h):
        block = lax.rem(c + n_c - s + 1, n_c) if way == 0 else lax.rem(c + s - 1, n_c)
        to = lax.rem(c + 1, n_c) if way == 0 else lax.rem(c + n_c - 1, n_c)
        dst = held.at[slot(block), at(h)]
        src = panel.at[at(h)] if s == 1 else dst
        return remote(src, dst, ring_s.at[way, s - 1, h], ring_r.at[way, s - 1, h], col=to)

    def ring_parts(s):
        return [(0, 0), (1, 1)] + ([(0, 1), (1, 0)] if s < half else [])

    def deep(step, h):
        block = lax.rem(c + n_c - step, n_c)
        to = taker(block)
        index = block * n_d + d - n_c * to
        src = panel.at[at(h)] if step == 0 else held.at[slot(block), at(h)]
        where = step + half - 1
        return to, remote(
            src, held.at[index, at(h)], deep_s.at[where, h], deep_r.at[index, h], depth=to
        )

    def start_deep(step, h):
        to, copy = deep(step, h)

        @pl.when(to != d)
        def _():
            copy.start()

    def own_copy():
        return pltpu.make_async_copy(panel, held.at[slot(c)], own_s)

    for way, h in ring_parts(1):
        ring(way, 1, h).start()
    for h in range(2):
        start_deep(0, h)

    @pl.when(taker(c) == d)
    def _():
        own_copy().start()

    def arrived(s, parts):
        for way, h in parts:
            ring(way, s, h).wait_recv()
            if s < half and (s + 1 < half or way == h):
                ring(way, s + 1, h).start()
            step = s if (way == 0 or s == half) else -s
            start_deep(step, h)

    def between(k, later):
        def when(point, action):
            if point % 2 == later:
                pl.when(k == point // 2)(action)

        when(1, window_second)
        when(3, window_third)
        if half > 1:
            when(2, lambda: arrived(1, ring_parts(1)[:2]))
            when(6, lambda: arrived(1, ring_parts(1)[2:]))

    every = pieces.at[pl.ds(0, total - 1)]
    pltpu.make_async_copy(every, every, diag_r).wait()
    mine = diag_ref.shape[0]
    for p in range(total):
        work[p * mine : (p + 1) * mine, :] = pieces[p]
    factor_all(work, low, inv, between)

    for s in range(2 if half > 1 else 1, half + 1):
        arrived(s, ring_parts(s))

    @pl.when(r != 0)
    def _():
        pltpu.make_async_copy(window, window, w3_r).wait()

    for j in range(n_c):
        q = n_c * d + j

        @pl.when(lax.rem(q, n_d) != d)
        def _(j=j):
            for h in range(2):
                landed = held.at[j, at(h)]
                pltpu.make_async_copy(landed, landed, deep_r.at[j, h]).wait()

    pltpu.make_async_copy(every, every, diag_s).wait()
    for s in range(1, half + 1):
        for way, h in ring_parts(s):
            ring(way, s, h).wait_send()
    for step in range(1 - half, half + 1):
        for h in range(2):
            to, copy = deep(step, h)

            @pl.when(to != d)
            def _(copy=copy):
                copy.wait_send()

    @pl.when(taker(c) == d)
    def _():
        own_copy().wait()

    for p, b, lo, count in window_parts():
        if p != b * n_d:
            @pl.when(position == p)
            def _(p=p, b=b, lo=lo, count=count):
                part(p, b, lo, count).wait_send()

    @pl.when(root)
    def _():
        for k in range(1, n_d):
            to_depth(k).wait_send()

    @pl.when(r == 0)
    def _():
        for k in range(1, n_r):
            to_row(k).wait_send()


def exchange_call(sizes, diag_block, panel, win_units):
    n_r, n_c, n_d = sizes
    total = n_r * n_c * n_d
    units, unit, width = panel.shape
    n = diag_block.shape[1]
    square = jax.ShapeDtypeStruct((n, n), jnp.float32)
    vmem, anywhere = pl.BlockSpec(memory_space=pltpu.VMEM), pl.BlockSpec(memory_space=pl.ANY)
    dma, owners = pltpu.SemaphoreType.DMA, -(-n_c * win_units // units)
    sems = [
        dma, dma, dma((2, n_c // 2, 2)), dma((2, n_c // 2, 2)), dma((n_c, 2)), dma((n_c, 2)),
        dma((owners, n_c)), dma((owners,)), dma((n_d,)), dma, dma((n_r,)), dma, dma,
    ]
    return pl.pallas_call(
        functools.partial(exchange, sizes, (0, units // 2, units), win_units),
        out_shape=(
            square,
            square,
            jax.ShapeDtypeStruct((2 * n_c, units, unit, width), jnp.float32),
            jax.ShapeDtypeStruct((win_units, unit, width), jnp.float32),
        ),
        in_specs=[vmem, vmem],
        out_specs=(vmem, vmem, anywhere, anywhere),
        scratch_shapes=[
            pltpu.VMEM((total, diag_block.shape[0], n), jnp.float32),
            pltpu.VMEM((n, n), jnp.float32),
            sems,
        ],
        compiler_params=pltpu.CompilerParams(has_side_effects=True),
    )(diag_block, panel)


def body(sizes, diag_block, panel_rows, trailing):
    n_r, n_c, n_d = sizes
    position = (lax.axis_index("row") * n_c + lax.axis_index("col")) * n_d + lax.axis_index("depth")
    mine = diag_block.shape[0]
    own_rows, win_rows = trailing.shape
    rows, width = panel_rows.shape
    unit = math.gcd(rows, win_rows)
    low, inv, held, window = exchange_call(
        sizes, diag_block, panel_rows.reshape(rows // unit, unit, width), win_rows // unit
    )
    owned = held[:n_c].reshape(own_rows, width)
    own_factor = lax.dynamic_slice_in_dim(low, position * mine, mine, 0)
    solved = dot(panel_rows, inv, 1, 1)
    weight = dot(dot(window.reshape(win_rows, width), inv, 1, 1), inv, 1, 0)
    updated = trailing - dot(owned, weight, 1, 1)
    return (own_factor, solved, updated)


def solution(mesh):
    sizes = tuple(mesh.shape[axis] for axis in AXES)
    specs = (P(AXES, None), P(AXES, None), P(("row", "depth"), "col"))
    return jax.shard_map(
        functools.partial(body, sizes), mesh=mesh, in_specs=specs, out_specs=specs, check_vma=False
    )
```

time: 352 us -> 238 us (0.68)
  waiting for transfers between devices: 257 us -> 0 us
  Pallas kernels: 55.8 us -> 213 us
  between operations: 13.8 us -> 0.69 us
  local copies, waits for them, and re-layouts: 1.47 us -> 5.9 us
    all_gather x2 -> x0, waiting for transfers between devices: 229 us -> none  [the longest x1 173 us: body(): block_row = lax.all_gather(panel_rows, ('col', 'depth'), axis=0, tiled=True)]
    pallas_call x1, Pallas kernels: 55.8 us -> 213 us  [exchange_call(): pl.pallas_call(functools.partial(exchange, sizes, (0, units // 2, units),...]
    psum x1 -> x0, waiting for transfers between devices: 27 us -> none  [spread(): return lax.psum(kept, axis)]
    slice x0 -> x1, local copies, waits for them, and re-layouts: none -> 4.48 us  [body(): owned = held[:n_c].reshape(own_rows, width)]
  transfers between devices with their start and end apart: 3 -> 0, of which waited for: 3 -> 0; matrix products, arithmetic and copies ran while one was open for 2% -> 0% of each run, Pallas kernels for 16% -> 0%
where the time goes in v2:
time: 238 us
  Pallas kernels  213 us (89%)
  matrix products  18.1 us (8%)
  local copies, waits for them, and re-layouts  5.9 us (2%)
    pallas_call x1, Pallas kernels, exchange_call(): pl.pallas_call(functools.partial(exchange, sizes, (0, units // 2, units),...  213 us
    dot_general x4, matrix products, dot(): lax.dot_general(left, right, (((left_dim,), (right_dim,)), ((), ())), pre...  18.1 us

profile of v2, /device:TPU:16, one launch (start us, length us, event | category | flops | bytes accessed | tf_op | source)
XLA Modules:
  0.0 237.5 jit_solution(16898087665213697888)
XLA Ops:
  0.6 212.9 %shard_map.58 = (f32[512,512]{1,0:T(8,128)}, f32[512,512]{1,0:T(8,128)}, f32[8,63,16,512]{3,2,1,0:T(8,128)}, f32[16,16,512]{2,1,0:T(8,128)}) custom-call(f32[16,512]{1,0:T(8,128)} %diag_ref.1, f32[63,16,512]{2,1,0:T(8,128)} %bitcast.14), custom_call_target="tpu_custom_call" | custom-call | tf_op jit(solution)/shard_map/pallas_call | solution.py:291
  213.5 1.4 constant_dynamic-slice_fusion
  214.9 2.4 %fusion = f32[256,512]{1,0:T(8,128)S(1)} fusion(f32[256,512]{1,0:T(8,128)} %bitcast.15, f32[512,512]{1,0:T(8,128)} %get-tuple-element.8), kind=kOutput, calls=%fused_computation.3 | convolution fusion | flops 805306368 | bytes 2097152 | tf_op jit(solution)/shard_map/dot_general | solution.py:17
  217.4 2.3 fusion.1
  219.6 0.0 copy-start
  219.7 4.5 %slice.3 = f32[4,63,16,512]{3,2,1,0:T(8,128)S(1)} slice(f32[8,63,16,512]{3,2,1,0:T(8,128)} %get-tuple-element.9), slice={[0:4], [0:63], [0:16], [0:512]} | slice | bytes 16515072 | tf_op jit(solution)/shard_map/slice | solution.py:320
  224.1 0.0 copy-done
  224.2 0.0 copy-start.1
  224.2 0.0 copy-start.2
  224.2 8.6 %convolution_subtract_fusion = f32[4032,256]{1,0:T(8,128)} fusion(f32[4032,256]{1,0:T(8,128)S(1)} %copy-done, f32[4032,512]{1,0:T(8,128)S(1)} %bitcast.13, f32[256,512]{1,0:T(8,128)S(1)} %fusion.1), kind=kOutput, calls=%fused_computation | convolution fusion | flops 6342819840 | bytes 17039360 | tf_op jit(solution)/shard_map/dot_general | solution.py:17
  232.8 0.0 copy-done.1
  232.8 0.0 copy-done.2
  232.8 4.8 %convolution_bitcast_fusion = f32[1008,512]{1,0:T(8,128)} fusion(f32[512,512]{1,0:T(8,128)S(1)} %copy-done.1, f32[1008,512]{1,0:T(8,128)S(1)} %copy-done.2), kind=kOutput, calls=%fused_computation.1 | convolution fusion | flops 3170893824 | bytes 5177344 | tf_op jit(solution)/shard_map/dot_general | solution.py:17
Async XLA Ops:
  219.6 4.5 %copy-start = (f32[4032,256]{1,0:T(8,128)S(1)}, f32[4032,256]{1,0:T(8,128)}, u32[]{:S(2)}) copy-start(f32[4032,256]{1,0:T(8,128)} %param.5) | copy-start | bytes 12386308
  224.2 8.6 %copy-start.1 = (f32[512,512]{1,0:T(8,128)S(1)}, f32[512,512]{1,0:T(8,128)}, u32[]{:S(2)}) copy-start(f32[512,512]{1,0:T(8,128)} %get-tuple-element.8) | copy-start | bytes 3145732
  224.2 8.6 %copy-start.2 = (f32[1008,512]{1,0:T(8,128)S(1)}, f32[1008,512]{1,0:T(8,128)}, u32[]{:S(2)}) copy-start(f32[1008,512]{1,0:T(8,128)} %param.4) | copy-start | bytes 6193156

commit v3 on v2

--- a/solution.py
+++ b/solution.py
@@ -72,7 +72,7 @@
     lax.fori_loop(0, n // LANES, step, 0)
 
 
-def exchange(sizes, cuts, win_units, diag_ref, panel, low, inv, held, window, pieces, work, sems):
+def exchange(sizes, cuts, win_units, diag_ref, panel, low, weight, solved, held, window, pieces, work, inv, sems):
     n_r, n_c, n_d = sizes
     total = n_r * n_c * n_d
     half = n_c // 2
@@ -227,12 +227,14 @@
         work[p * mine : (p + 1) * mine, :] = pieces[p]
     factor_all(work, low, inv, between)
 
+    @pl.when(r != 0)
+    def _():
+        pltpu.make_async_copy(window, window, w3_r).wait()
+
+    weight[...] = dot(dot(window[...].reshape(weight.shape), inv[...], 1, 1), inv[...], 1, 0)
+    solved[...] = dot(panel[...].reshape(solved.shape), inv[...], 1, 1)
     for s in range(2 if half > 1 else 1, half + 1):
         arrived(s, ring_parts(s))
-
-    @pl.when(r != 0)
-    def _():
-        pltpu.make_async_copy(window, window, w3_r).wait()
 
     for j in range(n_c):
         q = n_c * d + j
@@ -292,19 +294,42 @@
         functools.partial(exchange, sizes, (0, units // 2, units), win_units),
         out_shape=(
             square,
-            square,
+            jax.ShapeDtypeStruct((win_units * unit, width), jnp.float32),
+            jax.ShapeDtypeStruct((units * unit, width), jnp.float32),
             jax.ShapeDtypeStruct((2 * n_c, units, unit, width), jnp.float32),
-            jax.ShapeDtypeStruct((win_units, unit, width), jnp.float32),
         ),
         in_specs=[vmem, vmem],
-        out_specs=(vmem, vmem, anywhere, anywhere),
+        out_specs=(vmem, vmem, vmem, anywhere),
         scratch_shapes=[
+            pltpu.VMEM((win_units, unit, width), jnp.float32),
             pltpu.VMEM((total, diag_block.shape[0], n), jnp.float32),
+            pltpu.VMEM((n, n), jnp.float32),
             pltpu.VMEM((n, n), jnp.float32),
             sems,
         ],
         compiler_params=pltpu.CompilerParams(has_side_effects=True),
     )(diag_block, panel)
+
+
+def update(held, weight, trailing, out):
+    out[...] = trailing[...] - dot(held[...], weight[...], 1, 1)
+
+
+def update_call(held, weight, trailing):
+    rows, columns = trailing.shape
+    width = held.shape[1]
+    chunk = max(m for m in range(8, 1025, 8) if rows % m == 0)
+    return pl.pallas_call(
+        update,
+        grid=(rows // chunk,),
+        out_shape=jax.ShapeDtypeStruct(trailing.shape, jnp.float32),
+        in_specs=[
+            pl.BlockSpec((chunk, width), lambda i: (i, 0)),
+            pl.BlockSpec((columns, width), lambda i: (0, 0)),
+            pl.BlockSpec((chunk, columns), lambda i: (i, 0)),
+        ],
+        out_specs=pl.BlockSpec((chunk, columns), lambda i: (i, 0)),
+    )(held, weight, trailing)
 
 
 def body(sizes, diag_block, panel_rows, trailing):
@@ -314,14 +339,11 @@
     own_rows, win_rows = trailing.shape
     rows, width = panel_rows.shape
     unit = math.gcd(rows, win_rows)
-    low, inv, held, window = exchange_call(
+    low, weight, solved, held = exchange_call(
         sizes, diag_block, panel_rows.reshape(rows // unit, unit, width), win_rows // unit
     )
-    owned = held[:n_c].reshape(own_rows, width)
     own_factor = lax.dynamic_slice_in_dim(low, position * mine, mine, 0)
-    solved = dot(panel_rows, inv, 1, 1)
-    weight = dot(dot(window.reshape(win_rows, width), inv, 1, 1), inv, 1, 0)
-    updated = trailing - dot(owned, weight, 1, 1)
+    updated = update_call(held.reshape(2 * n_c * rows, width), weight, trailing)
     return (own_factor, solved, updated)
 
 

time: 238 us -> 229 us (0.962)
  matrix products: 18.1 us -> 0 us
  Pallas kernels: 213 us -> 225 us
  local copies, waits for them, and re-layouts: 5.9 us -> 2.69 us
    dot_general x4 -> x0, matrix products: 18.1 us -> none  [dot(): lax.dot_general(left, right, (((left_dim,), (right_dim,)), ((), ())), pre...]
    pallas_call x0 -> x1, Pallas kernels: none -> 11.7 us  [update_call(): pl.pallas_call(update, grid=(rows // chunk,), out_shape=jax.ShapeDtypeStr...]
    slice x1 -> x0, local copies, waits for them, and re-layouts: 4.48 us -> none  [body(): owned = held[:n_c].reshape(own_rows, width)]
where the time goes in v3:
time: 229 us; the launch traced here: 228 us
  Pallas kernels  225 us (98%)
  local copies, waits for them, and re-layouts  2.69 us (1%)
    pallas_call x1, Pallas kernels, exchange_call(): pl.pallas_call(functools.partial(exchange, sizes, (0, units // 2, units),...  213 us
    pallas_call x1, Pallas kernels, update_call(): pl.pallas_call(update, grid=(rows // chunk,), out_shape=jax.ShapeDtypeStr...  11.7 us

profile of v3, /device:TPU:16, one launch (start us, length us, event | category | flops | bytes accessed | tf_op | source)
XLA Modules:
  0.0 228.4 jit_solution(11803670909469692245)
XLA Ops:
  0.6 213.4 %shard_map.58 = (f32[512,512]{1,0:T(8,128)}, f32[256,512]{1,0:T(8,128)}, f32[1008,512]{1,0:T(8,128)}, f32[8,63,16,512]{3,2,1,0:T(8,128)}) custom-call(f32[16,512]{1,0:T(8,128)} %diag_ref.1, f32[63,16,512]{2,1,0:T(8,128)} %bitcast.3), custom_call_target="tpu_custom_call" | custom-call | tf_op jit(solution)/shard_map/pallas_call | solution.py:293
  214.0 1.4 constant_dynamic-slice_fusion
  215.4 0.0 copy-start
  215.4 11.7 %shard_map.59 = f32[4032,256]{1,0:T(8,128)} custom-call(f32[8064,512]{1,0:T(8,128)} %bitcast.2, f32[256,512]{1,0:T(8,128)} %get-tuple-element.10.weight, f32[4032,256]{1,0:T(8,128)} %trailing.1), custom_call_target="tpu_custom_call" | custom-call | tf_op jit(solution)/shard_map/pallas_call | solution.py:322
  227.1 0.0 copy-done
  227.1 1.3 copy.7
Async XLA Ops:
  215.4 11.7 %copy-start = (f32[1008,512]{1,0:T(8,128)S(1)}, f32[1008,512]{1,0:T(8,128)}, u32[]{:S(2)}) copy-start(f32[1008,512]{1,0:T(8,128)} %get-tuple-element.15) | copy-start | bytes 6193156
